TPU v7x, 32 devices: a whole 2x2x4 slice. The times are simulated.
32 devices in a mesh: groups: 2 (over y), rows: 4 (over z), cols: 2 (over x), sub: 2 (over core).
Axes of the slice: x: 2, y: 2, z: 4, core: 2. Of those that a mesh axis runs over, the one named last changes fastest.
Arguments:
- stored_vectors: bfloat16 [3072, 8192], P(('cols', 'sub'), ('groups', 'rows')), parts along dimension 1, may hold values from -0.59765625 to 0.59765625
- previous_columns: bfloat16 [8192, 256], P(('groups', 'rows', 'cols', 'sub')), parts along dimension 0, may hold values from -3 to 3
- pivots: int32 [512], P('groups'), parts along dimension 0, may hold values from 0 to 4095, as said below
- diagonal: float32 [8192], P(('groups', 'rows', 'cols', 'sub')), parts along dimension 0, may hold values from 2 to 32
- ket_blocks: bfloat16 [128, 128, 256], P(('groups', 'rows', 'cols', 'sub')), parts along dimension 0, may hold values from -6 to 6
- shell_tags: int32 [128, 128], P(('groups', 'rows', 'cols', 'sub')), parts along dimension 0, may hold values from 0 to 3
- target_blocks: int32 [32, 4], P('groups'), parts along dimension 0, may hold values from 0 to 31, as said below
- block_counts: int32 [32], P('groups'), parts along dimension 0, may hold values from 0 to 4, as said below
- shell_norms: float32 [4], replicated, may hold values from 0.5 to 2
Outputs:
- new_vectors: bfloat16 [8192, 256], P(('groups', 'rows', 'cols', 'sub')), parts along dimension 0
- diag_out: float32 [8192], P(('groups', 'rows', 'cols', 'sub')), parts along dimension 0
- next_columns: bfloat16 [8192, 256], P(('groups', 'rows', 'cols', 'sub')), parts along dimension 0
There are 2 independent parts, one for each index of `groups`. A program takes and returns all parts, laid end to end along the dimension named above; an argument that names none is the same for every part. Nothing has to cross between parts.
Inputs may be any that keep to these rules, and one draw needn't show every extreme that they name: `pivots`: 256 distinct AO pairs. `target_blocks`: the used slots of all owners name every block of the 32 blocks exactly once; a used slot's block lies on a device with the owner's cols and sub indices (blocks g * 2 to g * 2 + 1 lie on the device of linear index g, rows slowest; owner o is the device of linear index o). At most 1 of one owner's used slots go to one device, and some owner reaches that in every draw. Entries of unused slots are arbitrary blocks. `block_counts`: some owner uses all 4 slots in every draw.
All inputs are finite; a program needn't handle non-finite values.
Results may differ from a plain program's by a relative error of at most 0.0004.
Values may be sent and summed in bfloat16 or wider, within the bound.
A program may use at most 64 MiB of HBM per device.

v0:
```python
import jax
import jax.numpy as jnp
from jax import lax
from jax.sharding import PartitionSpec as P


def slot_plan(row_targets, count, column_size, per_device):
    slot_count = row_targets.shape[0]
    slots = jnp.arange(slot_count, dtype=jnp.int32)
    valid = slots < count
    receiver = row_targets // (column_size * per_device)
    within = row_targets % per_device
    earlier = (
        (receiver[:, None] == receiver[None, :])
        & valid[:, None]
        & valid[None, :]
        & (slots[None, :] < slots[:, None])
    )
    ranking = jnp.sum(earlier.astype(jnp.int32), axis=1)
    return (valid, receiver, ranking, within)


def body(
    stored_vectors,
    previous_columns,
    pivots,
    diagonal,
    ket_blocks,
    shell_tags,
    target_blocks,
    block_counts,
    shell_norms,
):
    rows_here = previous_columns.shape[0]
    batch = previous_columns.shape[1]
    block_rows = ket_blocks.shape[1]
    slot_count = ket_blocks.shape[0]
    per_device = rows_here // block_rows
    band_rows = stored_vectors.shape[1]
    band_index = lax.axis_index("rows")
    device_index = lax.axis_index(("rows", "cols", "sub"))
    column_index = lax.axis_index(("cols", "sub"))
    column_size = lax.axis_size(("cols", "sub"))
    band_size = lax.axis_size("rows")
    peer_slots = (slot_count + band_size - 1) // band_size
    local_pivots = pivots - device_index * rows_here
    matches = jnp.arange(rows_here, dtype=jnp.int32)[:, None] == local_pivots[None, :]
    diag_terms = jnp.sum(jnp.where(matches, diagonal[:, None], jnp.float32(0.0)), axis=0)
    pivot_diag = lax.psum(diag_terms, ("rows", "cols", "sub"))
    band_pivots = pivots - band_index * band_rows
    inside = (band_pivots >= 0) & (band_pivots < band_rows)
    clamped = jnp.clip(band_pivots, 0, band_rows - 1)
    taken = jnp.take(stored_vectors, clamped, axis=1).astype(jnp.float32)
    picked = jnp.where(inside[None, :], taken, jnp.float32(0.0))
    pivot_rows = lax.psum(picked, "rows").astype(jnp.bfloat16)
    kinds = jnp.arange(shell_norms.shape[0], dtype=jnp.int32)
    factor = jnp.sum(
        jnp.where(shell_tags[..., None] == kinds, shell_norms, jnp.float32(0.0)), axis=-1
    )
    fresh = (ket_blocks.astype(jnp.float32) * factor[..., None]).astype(jnp.bfloat16)
    own_targets = lax.dynamic_index_in_dim(target_blocks, device_index, 0, keepdims=False)
    own_count = lax.dynamic_index_in_dim(block_counts, device_index, 0, keepdims=False)
    valid, receiver, ranking, within = slot_plan(own_targets, own_count, column_size, per_device)
    lines = jnp.arange(band_size * peer_slots, dtype=jnp.int32)[:, None]
    routing = (
        (lines // peer_slots == receiver[None, :])
        & (lines % peer_slots == ranking[None, :])
        & valid[None, :]
    ).astype(jnp.bfloat16)
    outgoing = jnp.dot(
        routing, fresh.reshape(slot_count, block_rows * batch), preferred_element_type=jnp.float32
    )
    outgoing = outgoing.astype(jnp.bfloat16).reshape(band_size, peer_slots, block_rows, batch)
    incoming = lax.all_to_all(outgoing, "rows", split_axis=0, concat_axis=0, tiled=True)
    sources = jnp.arange(band_size, dtype=jnp.int32) * column_size + column_index
    source_targets = jnp.take(target_blocks, sources, axis=0)
    source_counts = jnp.take(block_counts, sources, axis=0)
    plan_each = jax.vmap(
        lambda row_targets, count: slot_plan(row_targets, count, column_size, per_device)
    )
    source_valid, source_receiver, source_rank, source_within = plan_each(
        source_targets, source_counts
    )
    arriving = source_valid & (source_receiver == band_index)
    places = jnp.arange(per_device, dtype=jnp.int32)[:, None, None, None]
    peer_lines = jnp.arange(peer_slots, dtype=jnp.int32)[None, None, :, None]
    hits = (
        (source_within[None, :, None, :] == places)
        & (source_rank[None, :, None, :] == peer_lines)
        & arriving[None, :, None, :]
    )
    placement = (
        jnp.any(hits, axis=3).astype(jnp.bfloat16).reshape(per_device, band_size * peer_slots)
    )
    arranged = jnp.dot(
        placement,
        incoming.reshape(band_size * peer_slots, block_rows * batch),
        preferred_element_type=jnp.float32,
    )
    next_columns = arranged.astype(jnp.bfloat16).reshape(rows_here, batch)
    product = lax.psum_scatter(
        lax.dot_general(
            stored_vectors, pivot_rows, (((0,), (0,)), ((), ())), preferred_element_type=jnp.float32
        ),
        ("cols", "sub"),
        scatter_dimension=0,
        tiled=True,
    )
    residual_cols = previous_columns.astype(jnp.float32) - product
    scaled = residual_cols / jnp.sqrt(pivot_diag)[None, :]
    new_vectors = scaled.astype(jnp.bfloat16)
    diag_out = diagonal - jnp.sum(scaled * scaled, axis=1)
    return (new_vectors, diag_out, next_columns)


def solution(mesh):
    return jax.shard_map(
        body,
        mesh=mesh,
        in_specs=(
            P(("cols", "sub"), ("groups", "rows")),
            P(("groups", "rows", "cols", "sub"), None),
            P("groups"),
            P(("groups", "rows", "cols", "sub")),
            P(("groups", "rows", "cols", "sub"), None, None),
            P(("groups", "rows", "cols", "sub"), None),
            P("groups", None),
            P("groups"),
            P(),
        ),
        out_specs=(
            P(("groups", "rows", "cols", "sub"), None),
            P(("groups", "rows", "cols", "sub")),
            P(("groups", "rows", "cols", "sub"), None),
        ),
        check_vma=False,
    )
```

profile of v0, /device:TPU:0, one launch (start us, length us, event | category | flops | bytes accessed | tf_op | source)
XLA Modules:
  0.0 100.1 jit_solution(16816415105481037228)
XLA Ops:
  7.2 0.0 reduce-scatter.2.cloned.1.call-start
  7.2 0.0 copy-start.6
  7.2 1.7 %copy.26 = bf16[768,1024]{0,1:T(8,128)(2,1)S(1)} copy(bf16[768,1024]{1,0:T(8,128)(2,1)} %param.9) | data formatting | bytes 3145728 | tf_op args[0]
  9.0 0.0 copy-done.6
  9.0 1.2 %gather_fusion = bf16[256,768]{1,0:T(8,128)(2,1)S(1)} fusion(bf16[768,1024]{0,1:T(8,128)(2,1)S(1)} %copy.26, s32[1024]{0:T(1024)S(1)} %pad_clamp_fusion.1), kind=kCustom, calls=%fused_computation | custom fusion | bytes 787456 | tf_op jit(solution)/shard_map/jit(_take)/gather | solution.py:53
  10.2 0.0 copy-start.1
  10.2 0.2 select_bitcast_fusion
  10.4 37.4 %all-reduce.1 = bf16[768,256]{0,1:T(8,128)(2,1)S(1)} all-reduce(f32[768,256]{0,1:T(8,128)S(1)} %select_bitcast_fusion), channel_id=1, replica_groups=mesh['groups'=2,'rows'=4,'cols'=2,'sub'=2] {'rows'}, use_global_device_ids=true, to_apply=%region_0.1 | all-reduce | flops 196608 | bytes 1179648 | tf_op jit(solution)/shard_map/psum | solution.py:55
  47.8 0.0 copy-done.1
  47.8 0.0 copy-start.7
  47.8 0.0 copy-start.8
  47.9 0.0 copy-start.2
  47.9 1.6 %convolution_bitcast_fusion = f32[1024,256]{0,1:T(8,128)} fusion(bf16[768,1024]{1,0:T(8,128)(2,1)S(1)} %copy-done.1, bf16[768,256]{0,1:T(8,128)(2,1)S(1)} %all-reduce.1), kind=kOutput, calls=%fused_computation.5 | convolution fusion | flops 402653184 | bytes 3014656 | tf_op jit(solution)/shard_map/dot_general | solution.py:102
  49.4 0.0 copy-start.4
  49.4 0.0 copy-start
  49.4 0.0 reduce-scatter.2.cloned.1.call-update
  49.5 0.0 copy-done.7
  49.5 0.0 copy-done.8
  49.5 0.1 select_reduce_fusion.1
  49.6 0.0 copy-done.2
  49.6 0.0 copy-start.5
  49.6 0.0 copy-start.3
  49.6 0.1 fusion.1
  49.7 0.2 copy.30
  50.0 0.2 copy-done.4
  50.1 0.2 dynamic-slice_reduce_fusion
  50.3 0.0 copy-done
  50.3 0.6 dynamic_slice.9
  50.9 0.6 iota_compare_fusion.6
  51.6 0.2 convert_reduce_fusion.1
  51.8 0.3 convolution_convert_fusion
  52.1 0.7 copy.34
  52.8 3.4 %all-to-all-start = ((bf16[4,1,128,256]{3,2,1,0:T(8,128)(2,1)}), bf16[4,1,128,256]{3,2,1,0:T(8,128)(2,1)S(1)}, u32[]{:S(2)}, u32[]{:S(2)}) async-start(bf16[4,1,128,256]{3,2,1,0:T(8,128)(2,1)} %bitcast.26), calls=%async_computation.1 | async-start | bytes 524288 | tf_op jit(solution)/shard_map/all_to_all | solution.py:74
  56.2 0.1 copy.27
  56.3 0.6 gather_fusion.2
  57.0 0.6 gather_fusion.1
  57.6 0.1 compare_and_fusion
  57.6 0.2 convert_reduce_fusion
  57.9 0.0 copy-done.5
  57.9 0.1 select_reduce_fusion
  58.0 31.2 %psum.15 = f32[256]{0:T(256)S(1)} all-reduce(f32[256]{0:T(256)S(1)} %select_reduce_fusion), channel_id=1, replica_groups=mesh['groups'=2,'rows'=4,'cols'=2,'sub'=2] {'rows','cols','sub'}, use_global_device_ids=true, to_apply=%region_3.4 | all-reduce | flops 256 | bytes 2048 | tf_op jit(solution)/shard_map/psum | solution.py:49
  89.2 0.0 copy-done.3
  89.2 0.1 copy.25
  89.3 0.1 add_select_fusion.2
  89.4 0.2 fusion.4
  89.5 0.0 all-to-all-done
  89.6 0.2 copy.32
  89.8 0.3 convolution_convert_fusion.1
  90.1 0.7 reshape.328
  90.8 0.0 reduce-scatter.2.cloned.1.call-done
  90.8 1.1 %multiply_reduce_fusion = (f32[256]{0:T(256)S(1)}, bf16[256,256]{0,1:T(8,128)(2,1)S(1)}) fusion(f32[256]{0:T(256)S(1)} %sqrt.3, f32[256,256]{0,1:T(8,128)} %reduce-scatter.2.cloned.1.call-done, bf16[256,256]{0,1:T(8,128)(2,1)S(1)} %copy.25), kind=kLoop, calls=%fused_computation.11 | loop fusion | flops 392960 | bytes 526336 | tf_op jit(solution)/shard_map/reduce_sum | solution.py:112
  91.9 0.8 copy.29
  92.6 0.6 sub.35
  (11 shorter events, 0.1 us)
Async XLA Ops:
  7.2 83.6 %reduce-scatter.2.cloned.1.call-start = ((), (), s32[]{:S(2)}) async-start(), calls=%async_computation.2 | async-start | bytes 1310720 | tf_op jit(solution)/shard_map/reduce_scatter | solution.py:101
  7.2 1.7 %copy-start.6 = (s32[256]{0:T(256)S(1)}, s32[256]{0:T(256)}, u32[]{:S(2)}) copy-start(s32[256]{0:T(256)} %param.11) | copy-start | bytes 3076
  10.2 37.6 %copy-start.1 = (bf16[768,1024]{1,0:T(8,128)(2,1)S(1)}, bf16[768,1024]{1,0:T(8,128)(2,1)}, u32[]{:S(2)}) copy-start(bf16[768,1024]{1,0:T(8,128)(2,1)} %param.9) | copy-start | bytes 4718596
  47.8 1.6 %copy-start.7 = (s32[4,128]{1,0:T(4,128)S(1)}, s32[4,128]{1,0:T(4,128)}, u32[]{:S(2)}) copy-start(s32[4,128]{1,0:T(4,128)} %param.14) | copy-start | bytes 6148
  47.8 1.6 %copy-start.8 = (f32[4]{0:T(128)S(1)}, f32[4]{0:T(128)}, u32[]{:S(2)}) copy-start(f32[4]{0:T(128)} %param.17) | copy-start | bytes 52
  47.9 1.7 %copy-start.2 = (bf16[4,128,256]{2,1,0:T(8,128)(2,1)S(1)}, bf16[4,128,256]{2,1,0:T(8,128)(2,1)}, u32[]{:S(2)}) copy-start(bf16[4,128,256]{2,1,0:T(8,128)(2,1)} %param.13) | copy-start | bytes 786436
  49.4 0.7 copy-start.4
  49.4 0.9 copy-start
  49.6 8.3 %copy-start.5 = (f32[256]{0:T(256)S(1)}, f32[256]{0:T(256)}, u32[]{:S(2)}) copy-start(f32[256]{0:T(256)} %param.12) | copy-start | bytes 3076
  49.6 39.6 %copy-start.3 = (bf16[256,256]{1,0:T(8,128)(2,1)S(1)}, bf16[256,256]{1,0:T(8,128)(2,1)}, u32[]{:S(2)}) copy-start(bf16[256,256]{1,0:T(8,128)(2,1)} %param.10) | copy-start | bytes 393220
  52.8 36.7 %all-to-all-start = ((bf16[4,1,128,256]{3,2,1,0:T(8,128)(2,1)}), bf16[4,1,128,256]{3,2,1,0:T(8,128)(2,1)S(1)}, u32[]{:S(2)}, u32[]{:S(2)}) async-start(bf16[4,1,128,256]{3,2,1,0:T(8,128)(2,1)} %bitcast.26), calls=%async_computation.1 | async-start | bytes 524288 | tf_op jit(solution)/shard_map/all_to_all | solution.py:74
Sparse Core Ops, SparseCore 0:
  49.6 24.2 reduce-scatter.1
where the time goes:
time: 100 us
  blocking collectives  68.6 us (69%)
  between operations  14.3 us (14%)
  local copies, waits for them, and re-layouts  7.74 us (8%)
  other arithmetic  3.79 us (4%)
  starting transfers between devices  3.44 us (3%)
  matrix products  2.14 us (2%)
    psum x1, blocking collectives, body(): pivot_rows = lax.psum(picked, 'rows').astype(jnp.bfloat16)  37.4 us
    psum x1, blocking collectives, body(): pivot_diag = lax.psum(diag_terms, ('rows', 'cols', 'sub'))  31.2 us
    unnamed x25, local copies, waits for them, and re-layouts  4.02 us
    all_to_all x1, starting transfers between devices, body(): lax.all_to_all(outgoing, 'rows', split_axis=0, concat_axis=0, tiled=True)  3.4 us
  transfers between devices with their start and end apart: 2, of which 0 were waited for; matrix products, arithmetic and copies ran while one was open for 6% of the time, Pallas kernels for 0%

commit v1 on v0

--- a/solution.py
+++ b/solution.py
@@ -46,7 +46,7 @@
     local_pivots = pivots - device_index * rows_here
     matches = jnp.arange(rows_here, dtype=jnp.int32)[:, None] == local_pivots[None, :]
     diag_terms = jnp.sum(jnp.where(matches, diagonal[:, None], jnp.float32(0.0)), axis=0)
-    pivot_diag = lax.psum(diag_terms, ("rows", "cols", "sub"))
+    pivot_diag = lax.psum(lax.psum(diag_terms, ("cols", "sub")), "rows")
     band_pivots = pivots - band_index * band_rows
     inside = (band_pivots >= 0) & (band_pivots < band_rows)
     clamped = jnp.clip(band_pivots, 0, band_rows - 1)

time: 100 us -> 91 us (0.910)
  blocking collectives: 68.6 us -> 44.7 us
  waiting for transfers between devices: 0.02 us -> 13.1 us
  other arithmetic: 3.79 us -> 5.15 us
    psum x2, blocking collectives: 68.6 us -> 44.7 us  [body(): pivot_diag = lax.psum(lax.psum(diag_terms, ('cols', 'sub')), 'rows')]
    reduce_scatter x1, waiting for transfers between devices: 0.01 us -> 8.34 us  [body(): lax.psum_scatter(lax.dot_general(stored_vectors, pivot_rows, (((0,), (0,)...]
    all_to_all x1, waiting for transfers between devices: 0.01 us -> 4.73 us  [body(): lax.all_to_all(outgoing, 'rows', split_axis=0, concat_axis=0, tiled=True)]
  transfers between devices with their start and end apart: 2 -> 2, of which waited for: 0 -> 2; matrix products, arithmetic and copies ran while one was open for 6% -> 7% of each run, Pallas kernels for 0% -> 0%
where the time goes in v1:
time: 91 us; the launch traced here: 90.6 us
  blocking collectives  44.7 us (49%)
  between operations  14.3 us (16%)
  waiting for transfers between devices  13.1 us (14%)
  local copies, waits for them, and re-layouts  7.77 us (9%)
  other arithmetic  5.15 us (6%)
  starting transfers between devices  3.45 us (4%)
  matrix products  2.14 us (2%)
    psum x2, blocking collectives, body(): pivot_diag = lax.psum(lax.psum(diag_terms, ('cols', 'sub')), 'rows')  44.7 us
    reduce_scatter x1, waiting for transfers between devices, body(): lax.psum_scatter(lax.dot_general(stored_vectors, pivot_rows, (((0,), (0,)...  8.34 us
    all_to_all x1, waiting for transfers between devices, body(): lax.all_to_all(outgoing, 'rows', split_axis=0, concat_axis=0, tiled=True)  4.73 us
    unnamed x25, local copies, waits for them, and re-layouts  4.05 us
    all_to_all x1, starting transfers between devices, body(): lax.all_to_all(outgoing, 'rows', split_axis=0, concat_axis=0, tiled=True)  3.41 us
  transfers between devices with their start and end apart: 2, of which 2 were waited for; matrix products, arithmetic and copies ran while one was open for 7% of the time, Pallas kernels for 0%

profile of v1, /device:TPU:0, one launch (start us, length us, event | category | flops | bytes accessed | tf_op | source)
XLA Modules:
  0.0 90.6 jit_solution(8050391367534933791)
XLA Ops:
  7.2 0.0 reduce-scatter.2.cloned.1.call-start
  7.2 0.7 broadcast_subtract_fusion
  7.9 0.8 select_reduce_fusion
  8.7 8.4 %psum.22 = f32[256]{0:T(256)S(1)} all-reduce(f32[256]{0:T(256)S(1)} %select_reduce_fusion), channel_id=1, replica_groups=mesh['groups'=2,'rows'=4,'cols'=2,'sub'=2] {'cols','sub'}, use_global_device_ids=true, to_apply=%region_3.4 | all-reduce | flops 256 | bytes 2048 | tf_op jit(solution)/shard_map/psum | solution.py:49
  17.1 0.0 copy-start.6
  17.1 1.7 %copy.26 = bf16[768,1024]{0,1:T(8,128)(2,1)S(1)} copy(bf16[768,1024]{1,0:T(8,128)(2,1)} %param.9) | data formatting | bytes 3145728 | tf_op args[0]
  18.8 0.0 copy-done.6
  18.8 1.2 %gather_fusion = bf16[256,768]{1,0:T(8,128)(2,1)S(1)} fusion(bf16[768,1024]{0,1:T(8,128)(2,1)S(1)} %copy.26, s32[1024]{0:T(1024)S(1)} %pad_clamp_fusion.1), kind=kCustom, calls=%fused_computation | custom fusion | bytes 787456 | tf_op jit(solution)/shard_map/jit(_take)/gather | solution.py:53
  20.0 0.0 copy-start.1
  20.0 0.2 select_bitcast_fusion
  20.2 36.4 %all-reduce.2 = (f32[256]{0:T(256)S(1)}, bf16[768,256]{0,1:T(8,128)(2,1)S(1)}) all-reduce(f32[256]{0:T(256)S(1)} %psum.22, f32[768,256]{0,1:T(8,128)S(1)} %select_bitcast_fusion), channel_id=1, replica_groups=mesh['groups'=2,'rows'=4,'cols'=2,'sub'=2] {'rows'}, use_global_device_ids=true, to_apply=%region_4.5 | all-reduce | flops 196864 | bytes 1181696 | tf_op jit(solution)/shard_map/psum | solution.py:49
  56.6 0.0 copy-done.1
  56.6 0.0 copy-start.7
  56.6 0.0 copy-start.8
  56.6 0.0 copy-start.2
  56.6 1.6 %convolution_bitcast_fusion = f32[1024,256]{0,1:T(8,128)} fusion(bf16[768,1024]{1,0:T(8,128)(2,1)S(1)} %copy-done.1, bf16[768,256]{0,1:T(8,128)(2,1)S(1)} %get-tuple-element.18), kind=kOutput, calls=%fused_computation.5 | convolution fusion | flops 402653184 | bytes 3014656 | tf_op jit(solution)/shard_map/dot_general | solution.py:102
  58.2 0.0 copy-start.4
  58.2 0.0 copy-start
  58.2 0.0 reduce-scatter.2.cloned.1.call-update
  58.2 0.0 copy-done.7
  58.2 0.0 copy-done.8
  58.3 0.1 select_reduce_fusion.1
  58.3 0.0 copy-done.2
  58.3 0.0 copy-start.3
  58.4 0.1 fusion.1
  58.5 0.2 copy.30
  58.7 0.2 copy-done.4
  58.9 0.2 dynamic-slice_reduce_fusion
  59.1 0.0 copy-done
  59.1 0.6 dynamic_slice.9
  59.7 0.6 iota_compare_fusion.6
  60.4 0.2 convert_reduce_fusion.1
  60.5 0.3 convolution_convert_fusion
  60.8 0.7 copy.34
  61.6 3.4 %all-to-all-start = ((bf16[4,1,128,256]{3,2,1,0:T(8,128)(2,1)}), bf16[4,1,128,256]{3,2,1,0:T(8,128)(2,1)S(1)}, u32[]{:S(2)}, u32[]{:S(2)}) async-start(bf16[4,1,128,256]{3,2,1,0:T(8,128)(2,1)} %bitcast.26), calls=%async_computation.1 | async-start | bytes 524288 | tf_op jit(solution)/shard_map/all_to_all | solution.py:74
  65.0 0.0 copy-start.5
  65.0 0.1 copy.27
  65.1 0.6 gather_fusion.2
  65.8 0.6 gather_fusion.1
  66.3 0.1 compare_and_fusion
  66.4 0.2 convert_reduce_fusion
  66.7 0.0 copy-done.3
  66.7 0.1 copy.25
  66.8 0.1 add_select_fusion.2
  66.9 0.2 fusion.4
  67.0 4.7 %all-to-all-done = bf16[4,1,128,256]{3,2,1,0:T(8,128)(2,1)S(1)} async-done(((bf16[4,1,128,256]{3,2,1,0:T(8,128)(2,1)}), bf16[4,1,128,256]{3,2,1,0:T(8,128)(2,1)S(1)}, u32[]{:S(2)}, u32[]{:S(2)}) %all-to-all-start) | async-done | bytes 262176 | tf_op jit(solution)/shard_map/all_to_all | solution.py:74
  71.8 0.2 copy.32
  72.0 0.3 convolution_convert_fusion.1
  72.3 0.7 reshape.328
  73.0 8.3 %reduce-scatter.2.cloned.1.call-done = f32[256,256]{0,1:T(8,128)} async-done(((f32[1024,256]{0,1:T(8,128)}), f32[256,256]{0,1:T(8,128)}) %reduce-scatter.2.cloned.1.call-update) | async-done | bytes 262160 | tf_op jit(solution)/shard_map/reduce_scatter | solution.py:101
  81.3 1.1 %multiply_reduce_fusion = (f32[256]{0:T(256)S(1)}, bf16[256,256]{0,1:T(8,128)(2,1)S(1)}) fusion(f32[256]{0:T(256)S(1)} %sqrt.3, f32[256,256]{0,1:T(8,128)} %reduce-scatter.2.cloned.1.call-done, bf16[256,256]{0,1:T(8,128)(2,1)S(1)} %copy.25), kind=kLoop, calls=%fused_computation.11 | loop fusion | flops 392960 | bytes 526336 | tf_op jit(solution)/shard_map/reduce_sum | solution.py:112
  82.4 0.8 copy.29
  83.2 0.0 copy-done.5
  83.2 0.6 sub.35
  (10 shorter events, 0.1 us)
Async XLA Ops:
  7.2 74.2 %reduce-scatter.2.cloned.1.call-start = ((), (), s32[]{:S(2)}) async-start(), calls=%async_computation.2 | async-start | bytes 1310720 | tf_op jit(solution)/shard_map/reduce_scatter | solution.py:101
  17.1 1.7 %copy-start.6 = (s32[256]{0:T(256)S(1)}, s32[256]{0:T(256)}, u32[]{:S(2)}) copy-start(s32[256]{0:T(256)} %param.11) | copy-start | bytes 3076
  20.0 36.6 %copy-start.1 = (bf16[768,1024]{1,0:T(8,128)(2,1)S(1)}, bf16[768,1024]{1,0:T(8,128)(2,1)}, u32[]{:S(2)}) copy-start(bf16[768,1024]{1,0:T(8,128)(2,1)} %param.9) | copy-start | bytes 4718596
  56.6 1.6 %copy-start.7 = (s32[4,128]{1,0:T(4,128)S(1)}, s32[4,128]{1,0:T(4,128)}, u32[]{:S(2)}) copy-start(s32[4,128]{1,0:T(4,128)} %param.14) | copy-start | bytes 6148
  56.6 1.6 %copy-start.8 = (f32[4]{0:T(128)S(1)}, f32[4]{0:T(128)}, u32[]{:S(2)}) copy-start(f32[4]{0:T(128)} %param.17) | copy-start | bytes 52
  56.6 1.7 %copy-start.2 = (bf16[4,128,256]{2,1,0:T(8,128)(2,1)S(1)}, bf16[4,128,256]{2,1,0:T(8,128)(2,1)}, u32[]{:S(2)}) copy-start(bf16[4,128,256]{2,1,0:T(8,128)(2,1)} %param.13) | copy-start | bytes 786436
  58.2 0.7 copy-start.4
  58.2 0.9 copy-start
  58.3 8.3 %copy-start.3 = (bf16[256,256]{1,0:T(8,128)(2,1)S(1)}, bf16[256,256]{1,0:T(8,128)(2,1)}, u32[]{:S(2)}) copy-start(bf16[256,256]{1,0:T(8,128)(2,1)} %param.10) | copy-start | bytes 393220
  61.6 10.2 %all-to-all-start = ((bf16[4,1,128,256]{3,2,1,0:T(8,128)(2,1)}), bf16[4,1,128,256]{3,2,1,0:T(8,128)(2,1)S(1)}, u32[]{:S(2)}, u32[]{:S(2)}) async-start(bf16[4,1,128,256]{3,2,1,0:T(8,128)(2,1)} %bitcast.26), calls=%async_computation.1 | async-start | bytes 524288 | tf_op jit(solution)/shard_map/all_to_all | solution.py:74
  65.0 18.2 %copy-start.5 = (f32[256]{0:T(256)S(1)}, f32[256]{0:T(256)}, u32[]{:S(2)}) copy-start(f32[256]{0:T(256)} %param.12) | copy-start | bytes 3076
Sparse Core Ops, SparseCore 0:
  58.4 22.9 reduce-scatter.1
